TPU v7x, 32 devices: a whole 2x2x4 slice. The times are simulated.
32 devices in a mesh: dp: 8 (over z, x), rep: 4 (over y, core).
Axes of the slice: x: 2, y: 2, z: 4, core: 2. Of those that a mesh axis runs over, the one named last changes fastest.
Arguments:
- tokens: bfloat16 [65536, 1280], P(('dp', 'rep')), may hold values from -6 to 6
- sketch_map: bfloat16 [65536, 128], P(('dp', 'rep')), may hold values from -0.125 to 0.125
- test_matrix: bfloat16 [4, 1024, 128], P('rep'), may hold values from -0.09375 to 0.09375
Outputs:
- basis: float32 [1280, 128], P('dp')
- factor: float32 [128, 128], replicated
All inputs are finite; a program needn't handle non-finite values.
Results may differ from a plain program's by a relative error of at most 0.0051.
Values may be sent and summed in bfloat16 or wider, within the bound.
A program may use at most 64 MiB of HBM per device.

v0:
```python
import jax
import jax.numpy as jnp
from jax import lax
from jax.sharding import PartitionSpec as P

ITERS = 2


def whole_factor(matrix):
    gram = jnp.dot(
        matrix.T, matrix, precision=lax.Precision.HIGHEST, preferred_element_type=jnp.float32
    )
    lower = jnp.linalg.cholesky(gram)
    return (jax.scipy.linalg.solve_triangular(lower, matrix.T, lower=True).T, lower.T)


def body(tokens, sketch_map, test_matrix):
    width = tokens.shape[1]
    strip = width // lax.axis_size("dp")
    total_tokens = tokens.shape[0] * lax.axis_size("dp") * lax.axis_size("rep")
    sketch = lax.dot_general(
        sketch_map, tokens, (((0,), (0,)), ((), ())), preferred_element_type=jnp.float32
    ).astype(jnp.bfloat16)
    merged = lax.all_to_all(sketch, "dp", split_axis=1, concat_axis=0, tiled=True)
    local_start = lax.dot_general(
        merged, test_matrix[0], (((0,), (0,)), ((), ())), preferred_element_type=jnp.float32
    )
    start = lax.psum(local_start, "rep")
    gathered = lax.all_gather(start, "dp", axis=0, tiled=True)
    current, factor = whole_factor(gathered)
    for step in range(ITERS):
        rounded = current.astype(jnp.bfloat16)
        projected = jnp.dot(tokens, rounded, preferred_element_type=jnp.float32).astype(
            jnp.bfloat16
        )
        local_sum = lax.dot_general(
            tokens, projected, (((0,), (0,)), ((), ())), preferred_element_type=jnp.float32
        )
        summed = lax.psum(local_sum, ("dp", "rep"))
        current, factor = whole_factor(summed / total_tokens)
    owned = lax.dynamic_slice_in_dim(current, lax.axis_index("dp") * strip, strip, 0)
    return (owned, factor)


def solution(mesh):
    return jax.shard_map(
        body,
        mesh=mesh,
        in_specs=(P(("dp", "rep"), None), P(("dp", "rep"), None), P("rep", None, None)),
        out_specs=(P("dp", None), P()),
        check_vma=False,
    )
```

profile of v0, /device:TPU:0, one launch (start us, length us, event | category | flops | bytes accessed | tf_op | source)
XLA Modules:
  0.0 453.5 jit_solution(7895339741333896489)
XLA Ops:
  7.2 1.0 copy-done
  8.2 3.4 convolution_convert_fusion.4
  11.8 18.0 %all_to_all.19 = bf16[128,8,160]{0,2,1:T(8,128)(2,1)S(1)} all-to-all(bf16[128,8,160]{0,2,1:T(8,128)(2,1)S(1)} %bitcast.66), channel_id=1, replica_groups=mesh['dp'=8,'rep'=4] {'dp'}, dimensions={1} | all-to-all | bytes 655360 | tf_op jit(solution)/shard_map/all_to_all | solution.py:24
  29.8 0.9 fusion.10
  30.7 28.8 %all-reduce.4.cloned.1.call-done = f32[160,128]{1,0:T(8,128)} async-done(((f32[160,128]{1,0:T(8,128)}), f32[160,128]{1,0:T(8,128)}) %all-reduce.4.cloned.1.call-update) | async-done | bytes 81936 | tf_op jit(solution)/shard_map/psum | solution.py:28
  59.5 32.0 %all_gather.3 = f32[1280,128]{1,0:T(8,128)S(1)} all-gather(f32[160,128]{1,0:T(8,128)} %all-reduce.4.cloned.1.call-done), channel_id=1, replica_groups=mesh['dp'=8,'rep'=4] {'dp'}, dimensions={0}, use_global_device_ids=true | all-gather | bytes 737280 | tf_op jit(solution)/shard_map/all_gather | solution.py:29
  91.5 1.2 fusion.36
  92.8 11.7 %cholesky.59 = f32[128,128]{1,0:T(8,128)S(1)} custom-call(f32[128,128]{1,0:T(8,128)S(1)} %fusion.25), custom_call_target="Cholesky" | custom-call | tf_op jit(solution)/shard_map/jit(cholesky)/cholesky | solution.py:13
  105.2 0.7 fusion.18
  105.9 9.8 %custom-call.7 = f32[1,128,128]{1,2,0:T(8,128)S(1)} custom-call(f32[1,128,128]{2,1,0:T(8,128)S(1)} %fusion.18), custom_call_target="InvertDiagBlocksLowerTriangular" | custom-call | tf_op jit(solution)/shard_map/jit(_solve_triangular)/triangular_solve | solution.py:14
  115.7 0.8 convolution_convert_fusion.3
  116.5 7.5 %convolution_bitcast_fusion.1 = f32[1280,128]{0,1:T(8,128)} fusion(bf16[2048,1280]{1,0:T(8,128)(2,1)} %param.6, bf16[128,1280]{1,0:T(8,128)(2,1)S(1)} %convolution_convert_fusion.3), kind=kOutput, calls=%fused_computation.1 | convolution fusion | flops 1342439424 | bytes 6225920 | tf_op jit(solution)/shard_map/dot_general | solution.py:36
  124.2 130.7 %all-reduce.6.cloned.1.call-done = f32[1280,128]{0,1:T(8,128)} async-done(((f32[1280,128]{0,1:T(8,128)}), f32[1280,128]{0,1:T(8,128)}) %all-reduce.6.cloned.1.call-update) | async-done | bytes 655376 | tf_op jit(solution)/shard_map/psum | solution.py:39
  255.0 2.0 fusion.8
  257.1 11.7 %cholesky.70 = f32[128,128]{1,0:T(8,128)S(1)} custom-call(f32[128,128]{1,0:T(8,128)S(1)} %fusion.23), custom_call_target="Cholesky" | custom-call | tf_op jit(solution)/shard_map/jit(cholesky)/cholesky | solution.py:13
  270.2 9.8 %custom-call.8 = f32[1,128,128]{1,2,0:T(8,128)S(1)} custom-call(f32[1,128,128]{2,1,0:T(8,128)S(1)} %fusion.19), custom_call_target="InvertDiagBlocksLowerTriangular" | custom-call | tf_op jit(solution)/shard_map/jit(_solve_triangular)/triangular_solve | solution.py:14
  280.0 1.8 convolution_convert_fusion.1
  281.8 7.5 %convolution_bitcast_fusion = f32[1280,128]{0,1:T(8,128)} fusion(bf16[2048,1280]{1,0:T(8,128)(2,1)} %param.6, bf16[128,1280]{1,0:T(8,128)(2,1)S(1)} %convolution_convert_fusion.1), kind=kOutput, calls=%fused_computation | convolution fusion | flops 1342439424 | bytes 6225920 | tf_op jit(solution)/shard_map/dot_general | solution.py:36
  289.3 128.8 %all-reduce.8.cloned.1.call-done = f32[1280,128]{0,1:T(8,128)} async-done(((f32[1280,128]{0,1:T(8,128)}), f32[1280,128]{0,1:T(8,128)}) %all-reduce.8.cloned.1.call-update) | async-done | bytes 655376 | tf_op jit(solution)/shard_map/psum | solution.py:39
  418.1 2.0 fusion.5
  420.2 11.9 %cholesky.81 = f32[128,128]{1,0:T(8,128)S(1)} custom-call(f32[128,128]{1,0:T(8,128)S(1)} %fusion.21), custom_call_target="Cholesky" | custom-call | tf_op jit(solution)/shard_map/jit(cholesky)/cholesky | solution.py:13
  433.5 9.8 %custom-call.9 = f32[1,128,128]{1,2,0:T(8,128)S(1)} custom-call(f32[1,128,128]{2,1,0:T(8,128)S(1)} %get-tuple-element.9), custom_call_target="InvertDiagBlocksLowerTriangular" | custom-call | tf_op jit(solution)/shard_map/jit(_solve_triangular)/triangular_solve | solution.py:14
  443.3 0.7 copy.14
  444.0 2.3 fusion
  (25 shorter events, 4.9 us)
Async XLA Ops:
  7.2 1.0 copy-start
  7.2 22.6 %copy-start.1 = (bf16[1,1024,128]{2,1,0:T(8,128)(2,1)S(1)}, bf16[1,1024,128]{2,1,0:T(8,128)(2,1)}, u32[]{:S(2)}) copy-start(bf16[1,1024,128]{2,1,0:T(8,128)(2,1)} %param.8) | copy-start | bytes 786436
  7.2 52.3 %all-reduce.4.cloned.1.call-start = ((), (), s32[]{:S(2)}) async-start(), calls=%async_computation.1 | async-start | bytes 163840 | tf_op jit(solution)/shard_map/psum | solution.py:28
  30.7 224.3 %all-reduce.6.cloned.1.call-start = ((), (), s32[]{:S(2)}) async-start(), calls=%async_computation.2 | async-start | bytes 1310720 | tf_op jit(solution)/shard_map/psum | solution.py:39
  124.0 294.1 %all-reduce.8.cloned.1.call-start = ((), (), s32[]{:S(2)}) async-start(), calls=%async_computation.3 | async-start | bytes 1310720 | tf_op jit(solution)/shard_map/psum | solution.py:39
Sparse Core Ops, SparseCore 0:
  30.8 28.6 all-reduce.3
  124.1 130.8 all-reduce.5
  289.5 128.6 all-reduce.7
where the time goes:
time: 454 us
  waiting for transfers between devices  288 us (63%)
  other arithmetic  68.8 us (15%)
  blocking collectives  50 us (11%)
  matrix products  29.3 us (6%)
  between operations  13.9 us (3%)
    psum x2, waiting for transfers between devices, body(): summed = lax.psum(local_sum, ('dp', 'rep'))  260 us
    another operation x9, other arithmetic, whole_factor(): lower = jnp.linalg.cholesky(gram)  37.4 us
    all_gather x1, blocking collectives, body(): gathered = lax.all_gather(start, 'dp', axis=0, tiled=True)  32 us
    another operation x5, other arithmetic, whole_factor(): jax.scipy.linalg.solve_triangular(lower, matrix.T, lower=True)  30.7 us
    psum x1, waiting for transfers between devices, body(): start = lax.psum(local_start, 'rep')  28.8 us
    all_to_all x1, blocking collectives, body(): lax.all_to_all(sketch, 'dp', split_axis=1, concat_axis=0, tiled=True)  18 us
    dot_general x2, matrix products, body(): lax.dot_general(tokens, projected, (((0,), (0,)), ((), ())), preferred_el...  15 us
  transfers between devices with their start and end apart: 3, of which 3 were waited for; matrix products, arithmetic and copies ran while one was open for 0% of the time, Pallas kernels for 0%

commit v1 on v0

--- a/solution.py
+++ b/solution.py
@@ -25,7 +25,7 @@
     local_start = lax.dot_general(
         merged, test_matrix[0], (((0,), (0,)), ((), ())), preferred_element_type=jnp.float32
     )
-    start = lax.psum(local_start, "rep")
+    start = jnp.sum(lax.all_gather(local_start, "rep"), axis=0)
     gathered = lax.all_gather(start, "dp", axis=0, tiled=True)
     current, factor = whole_factor(gathered)
     for step in range(ITERS):

time: 454 us -> 428 us (0.943)
  waiting for transfers between devices: 288 us -> 256 us
  blocking collectives: 50 us -> 55.9 us
    psum x1 -> x0, waiting for transfers between devices: 28.8 us -> none  [body(): start = lax.psum(local_start, 'rep')]
    all_gather x0 -> x1, blocking collectives: none -> 6.13 us  [body(): start = jnp.sum(lax.all_gather(local_start, 'rep'), axis=0)]
  transfers between devices with their start and end apart: 3 -> 2, of which waited for: 3 -> 2; matrix products, arithmetic and copies ran while one was open for 0% -> 0% of each run, Pallas kernels for 0% -> 0%
where the time goes in v1:
time: 428 us; the launch traced here: 427 us
  waiting for transfers between devices  256 us (60%)
  other arithmetic  68.8 us (16%)
  blocking collectives  55.9 us (13%)
  matrix products  28.7 us (7%)
  between operations  14.2 us (3%)
    psum x2, waiting for transfers between devices, body(): summed = lax.psum(local_sum, ('dp', 'rep'))  256 us
    another operation x9, other arithmetic, whole_factor(): lower = jnp.linalg.cholesky(gram)  37.4 us
    all_gather x1, blocking collectives, body(): gathered = lax.all_gather(start, 'dp', axis=0, tiled=True)  31.7 us
    another operation x5, other arithmetic, whole_factor(): jax.scipy.linalg.solve_triangular(lower, matrix.T, lower=True)  30.7 us
    all_to_all x1, blocking collectives, body(): lax.all_to_all(sketch, 'dp', split_axis=1, concat_axis=0, tiled=True)  18 us
    dot_general x2, matrix products, body(): lax.dot_general(tokens, projected, (((0,), (0,)), ((), ())), preferred_el...  15 us
  transfers between devices with their start and end apart: 2, of which 2 were waited for; matrix products, arithmetic and copies ran while one was open for 0% of the time, Pallas kernels for 0%

profile of v1, /device:TPU:0, one launch (start us, length us, event | category | flops | bytes accessed | tf_op | source)
XLA Modules:
  0.0 427.2 jit_solution(162333316408541677)
XLA Ops:
  7.2 1.0 copy-done
  8.2 3.4 convolution_convert_fusion.4
  11.8 18.0 %all_to_all.19 = bf16[128,8,160]{0,2,1:T(8,128)(2,1)S(1)} all-to-all(bf16[128,8,160]{0,2,1:T(8,128)(2,1)S(1)} %bitcast.68), channel_id=1, replica_groups=mesh['dp'=8,'rep'=4] {'dp'}, dimensions={1} | all-to-all | bytes 655360 | tf_op jit(solution)/shard_map/all_to_all | solution.py:24
  30.0 6.1 %all-gather = f32[640,128]{1,0:T(8,128)S(1)} all-gather(f32[160,128]{1,0:T(8,128)S(1)} %fusion.10), channel_id=2, replica_groups=mesh['dp'=8,'rep'=4] {'rep'}, dimensions={0}, use_global_device_ids=true | all-gather | bytes 409600 | tf_op jit(solution)/shard_map/all_gather | solution.py:28
  36.2 31.7 %all_gather.11 = f32[1280,128]{1,0:T(8,128)S(1)} all-gather(f32[160,128]{1,0:T(8,128)S(1)} %reduce_sum.9), channel_id=1, replica_groups=mesh['dp'=8,'rep'=4] {'dp'}, dimensions={0}, use_global_device_ids=true | all-gather | bytes 737280 | tf_op jit(solution)/shard_map/all_gather | solution.py:29
  67.9 1.2 fusion.36
  69.3 11.7 %cholesky.59 = f32[128,128]{1,0:T(8,128)S(1)} custom-call(f32[128,128]{1,0:T(8,128)S(1)} %fusion.25), custom_call_target="Cholesky" | custom-call | tf_op jit(solution)/shard_map/jit(cholesky)/cholesky | solution.py:13
  81.7 0.7 fusion.18
  82.3 9.8 %custom-call.7 = f32[1,128,128]{1,2,0:T(8,128)S(1)} custom-call(f32[1,128,128]{2,1,0:T(8,128)S(1)} %fusion.18), custom_call_target="InvertDiagBlocksLowerTriangular" | custom-call | tf_op jit(solution)/shard_map/jit(_solve_triangular)/triangular_solve | solution.py:14
  92.1 0.8 convolution_convert_fusion.3
  92.9 7.5 %convolution_bitcast_fusion.1 = f32[1280,128]{0,1:T(8,128)} fusion(bf16[2048,1280]{1,0:T(8,128)(2,1)} %param.6, bf16[128,1280]{1,0:T(8,128)(2,1)S(1)} %convolution_convert_fusion.3), kind=kOutput, calls=%fused_computation.1 | convolution fusion | flops 1342439424 | bytes 6225920 | tf_op jit(solution)/shard_map/dot_general | solution.py:36
  100.7 127.7 %all-reduce.3.cloned.1.call-done = f32[1280,128]{0,1:T(8,128)} async-done(((f32[1280,128]{0,1:T(8,128)}), f32[1280,128]{0,1:T(8,128)}) %all-reduce.3.cloned.1.call-update) | async-done | bytes 655376 | tf_op jit(solution)/shard_map/psum | solution.py:39
  228.3 2.0 fusion.8
  230.4 11.7 %cholesky.70 = f32[128,128]{1,0:T(8,128)S(1)} custom-call(f32[128,128]{1,0:T(8,128)S(1)} %fusion.23), custom_call_target="Cholesky" | custom-call | tf_op jit(solution)/shard_map/jit(cholesky)/cholesky | solution.py:13
  242.8 0.7 fusion.19
  243.5 9.8 %custom-call.8 = f32[1,128,128]{1,2,0:T(8,128)S(1)} custom-call(f32[1,128,128]{2,1,0:T(8,128)S(1)} %fusion.19), custom_call_target="InvertDiagBlocksLowerTriangular" | custom-call | tf_op jit(solution)/shard_map/jit(_solve_triangular)/triangular_solve | solution.py:14
  253.3 1.8 convolution_convert_fusion.1
  255.1 7.5 %convolution_bitcast_fusion = f32[1280,128]{0,1:T(8,128)} fusion(bf16[2048,1280]{1,0:T(8,128)(2,1)} %param.6, bf16[128,1280]{1,0:T(8,128)(2,1)S(1)} %convolution_convert_fusion.1), kind=kOutput, calls=%fused_computation | convolution fusion | flops 1342439424 | bytes 6225920 | tf_op jit(solution)/shard_map/dot_general | solution.py:36
  262.7 128.8 %all-reduce.5.cloned.1.call-done = f32[1280,128]{0,1:T(8,128)} async-done(((f32[1280,128]{0,1:T(8,128)}), f32[1280,128]{0,1:T(8,128)}) %all-reduce.5.cloned.1.call-update) | async-done | bytes 655376 | tf_op jit(solution)/shard_map/psum | solution.py:39
  391.4 2.0 fusion.5
  393.6 11.9 %cholesky.81 = f32[128,128]{1,0:T(8,128)S(1)} custom-call(f32[128,128]{1,0:T(8,128)S(1)} %fusion.21), custom_call_target="Cholesky" | custom-call | tf_op jit(solution)/shard_map/jit(cholesky)/cholesky | solution.py:13
  406.8 9.8 %custom-call.9 = f32[1,128,128]{1,2,0:T(8,128)S(1)} custom-call(f32[1,128,128]{2,1,0:T(8,128)S(1)} %get-tuple-element.9), custom_call_target="InvertDiagBlocksLowerTriangular" | custom-call | tf_op jit(solution)/shard_map/jit(_solve_triangular)/triangular_solve | solution.py:14
  416.6 0.7 copy.14
  417.4 2.3 fusion
  (24 shorter events, 4.4 us)
Async XLA Ops:
  7.2 1.0 copy-start
  7.2 22.6 %copy-start.1 = (bf16[1,1024,128]{2,1,0:T(8,128)(2,1)S(1)}, bf16[1,1024,128]{2,1,0:T(8,128)(2,1)}, u32[]{:S(2)}) copy-start(bf16[1,1024,128]{2,1,0:T(8,128)(2,1)} %param.8) | copy-start | bytes 786436
  7.2 221.1 %all-reduce.3.cloned.1.call-start = ((), (), s32[]{:S(2)}) async-start(), calls=%async_computation.1 | async-start | bytes 1310720 | tf_op jit(solution)/shard_map/psum | solution.py:39
  100.4 291.0 %all-reduce.5.cloned.1.call-start = ((), (), s32[]{:S(2)}) async-start(), calls=%async_computation.2 | async-start | bytes 1310720 | tf_op jit(solution)/shard_map/psum | solution.py:39
Sparse Core Ops, SparseCore 0:
  100.6 127.7 all-reduce.2
  262.8 128.6 all-reduce.4

commit v2 on v0

--- a/solution.py
+++ b/solution.py
@@ -36,7 +36,7 @@
         local_sum = lax.dot_general(
             tokens, projected, (((0,), (0,)), ((), ())), preferred_element_type=jnp.float32
         )
-        summed = lax.psum(local_sum, ("dp", "rep"))
+        summed = lax.psum(lax.psum(local_sum, "rep"), "dp")
         current, factor = whole_factor(summed / total_tokens)
     owned = lax.dynamic_slice_in_dim(current, lax.axis_index("dp") * strip, strip, 0)
     return (owned, factor)

time: 454 us -> 417 us (0.919)
  waiting for transfers between devices: 288 us -> 252 us
    psum x2 -> x4, waiting for transfers between devices: 260 us -> 223 us  [body(): summed = lax.psum(lax.psum(local_sum, 'rep'), 'dp')]
  transfers between devices with their start and end apart: 3 -> 5, of which waited for: 3 -> 5; matrix products, arithmetic and copies ran while one was open for 0% -> 0% of each run, Pallas kernels for 0% -> 0%
where the time goes in v2:
time: 417 us
  waiting for transfers between devices  252 us (60%)
  other arithmetic  68.6 us (16%)
  blocking collectives  50 us (12%)
  matrix products  29.4 us (7%)
  between operations  13.9 us (3%)
    psum x4, waiting for transfers between devices, body(): summed = lax.psum(lax.psum(local_sum, 'rep'), 'dp')  223 us
    another operation x9, other arithmetic, whole_factor(): lower = jnp.linalg.cholesky(gram)  37.2 us
    all_gather x1, blocking collectives, body(): gathered = lax.all_gather(start, 'dp', axis=0, tiled=True)  32 us
    another operation x5, other arithmetic, whole_factor(): jax.scipy.linalg.solve_triangular(lower, matrix.T, lower=True)  30.7 us
    psum x1, waiting for transfers between devices, body(): start = lax.psum(local_start, 'rep')  28.8 us
    all_to_all x1, blocking collectives, body(): lax.all_to_all(sketch, 'dp', split_axis=1, concat_axis=0, tiled=True)  18 us
    dot_general x2, matrix products, body(): lax.dot_general(tokens, projected, (((0,), (0,)), ((), ())), preferred_el...  15 us
  transfers between devices with their start and end apart: 5, of which 5 were waited for; matrix products, arithmetic and copies ran while one was open for 0% of the time, Pallas kernels for 0%

profile of v2, /device:TPU:0, one launch (start us, length us, event | category | flops | bytes accessed | tf_op | source)
XLA Modules:
  0.0 416.9 jit_solution(11257115136856673982)
XLA Ops:
  7.2 1.0 copy-done
  8.2 3.4 convolution_convert_fusion.4
  11.8 18.0 %all_to_all.19 = bf16[128,8,160]{0,2,1:T(8,128)(2,1)S(1)} all-to-all(bf16[128,8,160]{0,2,1:T(8,128)(2,1)S(1)} %bitcast.66), channel_id=1, replica_groups=mesh['dp'=8,'rep'=4] {'dp'}, dimensions={1} | all-to-all | bytes 655360 | tf_op jit(solution)/shard_map/all_to_all | solution.py:24
  29.8 0.9 fusion.10
  30.7 28.8 %all-reduce.6.cloned.1.call-done = f32[160,128]{1,0:T(8,128)} async-done(((f32[160,128]{1,0:T(8,128)}), f32[160,128]{1,0:T(8,128)}) %all-reduce.6.cloned.1.call-update) | async-done | bytes 81936 | tf_op jit(solution)/shard_map/psum | solution.py:28
  59.5 32.0 %all_gather.3 = f32[1280,128]{1,0:T(8,128)S(1)} all-gather(f32[160,128]{1,0:T(8,128)} %all-reduce.6.cloned.1.call-done), channel_id=1, replica_groups=mesh['dp'=8,'rep'=4] {'dp'}, dimensions={0}, use_global_device_ids=true | all-gather | bytes 737280 | tf_op jit(solution)/shard_map/all_gather | solution.py:29
  91.5 1.2 fusion.36
  92.8 11.7 %cholesky.59 = f32[128,128]{1,0:T(8,128)S(1)} custom-call(f32[128,128]{1,0:T(8,128)S(1)} %fusion.25), custom_call_target="Cholesky" | custom-call | tf_op jit(solution)/shard_map/jit(cholesky)/cholesky | solution.py:13
  105.9 9.8 %custom-call.7 = f32[1,128,128]{1,2,0:T(8,128)S(1)} custom-call(f32[1,128,128]{2,1,0:T(8,128)S(1)} %fusion.18), custom_call_target="InvertDiagBlocksLowerTriangular" | custom-call | tf_op jit(solution)/shard_map/jit(_solve_triangular)/triangular_solve | solution.py:14
  115.7 0.8 convolution_convert_fusion.3
  116.5 7.5 %convolution_bitcast_fusion.1 = f32[1280,128]{0,1:T(8,128)} fusion(bf16[2048,1280]{1,0:T(8,128)(2,1)} %param.6, bf16[128,1280]{1,0:T(8,128)(2,1)S(1)} %convolution_convert_fusion.3), kind=kOutput, calls=%fused_computation.1 | convolution fusion | flops 1342439424 | bytes 6225920 | tf_op jit(solution)/shard_map/dot_general | solution.py:36
  124.1 35.4 %all-reduce.8.cloned.1.call-done = f32[1280,128]{0,1:T(8,128)} async-done(((f32[1280,128]{0,1:T(8,128)}), f32[1280,128]{0,1:T(8,128)}) %all-reduce.8.cloned.1.call-update) | async-done | bytes 655376 | tf_op jit(solution)/shard_map/psum | solution.py:39
  159.7 76.9 %all-reduce.10.cloned.1.call-done = f32[1280,128]{0,1:T(8,128)} async-done(((f32[1280,128]{0,1:T(8,128)}), f32[1280,128]{0,1:T(8,128)}) %all-reduce.10.cloned.1.call-update) | async-done | bytes 655376 | tf_op jit(solution)/shard_map/psum | solution.py:39
  236.6 2.0 fusion.8
  238.8 11.7 %cholesky.70 = f32[128,128]{1,0:T(8,128)S(1)} custom-call(f32[128,128]{1,0:T(8,128)S(1)} %fusion.23), custom_call_target="Cholesky" | custom-call | tf_op jit(solution)/shard_map/jit(cholesky)/cholesky | solution.py:13
  251.8 9.8 %custom-call.8 = f32[1,128,128]{1,2,0:T(8,128)S(1)} custom-call(f32[1,128,128]{2,1,0:T(8,128)S(1)} %fusion.19), custom_call_target="InvertDiagBlocksLowerTriangular" | custom-call | tf_op jit(solution)/shard_map/jit(_solve_triangular)/triangular_solve | solution.py:14
  261.7 1.8 convolution_convert_fusion.1
  263.5 7.5 %convolution_bitcast_fusion = f32[1280,128]{0,1:T(8,128)} fusion(bf16[2048,1280]{1,0:T(8,128)(2,1)} %param.6, bf16[128,1280]{1,0:T(8,128)(2,1)S(1)} %convolution_convert_fusion.1), kind=kOutput, calls=%fused_computation | convolution fusion | flops 1342439424 | bytes 6225920 | tf_op jit(solution)/shard_map/dot_general | solution.py:36
  271.3 33.4 %all-reduce.12.cloned.1.call-done = f32[1280,128]{0,1:T(8,128)} async-done(((f32[1280,128]{0,1:T(8,128)}), f32[1280,128]{0,1:T(8,128)}) %all-reduce.12.cloned.1.call-update) | async-done | bytes 655376 | tf_op jit(solution)/shard_map/psum | solution.py:39
  304.7 77.0 %all-reduce.14.cloned.1.call-done = f32[1280,128]{0,1:T(8,128)} async-done(((f32[1280,128]{0,1:T(8,128)}), f32[1280,128]{0,1:T(8,128)}) %all-reduce.14.cloned.1.call-update) | async-done | bytes 655376 | tf_op jit(solution)/shard_map/psum | solution.py:39
  381.7 2.0 fusion.5
  383.8 11.7 %cholesky.81 = f32[128,128]{1,0:T(8,128)S(1)} custom-call(f32[128,128]{1,0:T(8,128)S(1)} %fusion.21), custom_call_target="Cholesky" | custom-call | tf_op jit(solution)/shard_map/jit(cholesky)/cholesky | solution.py:13
  396.9 9.8 %custom-call.9 = f32[1,128,128]{1,2,0:T(8,128)S(1)} custom-call(f32[1,128,128]{2,1,0:T(8,128)S(1)} %get-tuple-element.9), custom_call_target="InvertDiagBlocksLowerTriangular" | custom-call | tf_op jit(solution)/shard_map/jit(_solve_triangular)/triangular_solve | solution.py:14
  407.4 2.3 fusion
  (31 shorter events, 6.6 us)
Async XLA Ops:
  7.2 1.0 copy-start
  7.2 22.6 %copy-start.1 = (bf16[1,1024,128]{2,1,0:T(8,128)(2,1)S(1)}, bf16[1,1024,128]{2,1,0:T(8,128)(2,1)}, u32[]{:S(2)}) copy-start(bf16[1,1024,128]{2,1,0:T(8,128)(2,1)} %param.8) | copy-start | bytes 786436
  7.2 52.3 %all-reduce.6.cloned.1.call-start = ((), (), s32[]{:S(2)}) async-start(), calls=%async_computation.1 | async-start | bytes 163840 | tf_op jit(solution)/shard_map/psum | solution.py:28
  30.7 128.8 %all-reduce.8.cloned.1.call-start = ((), (), s32[]{:S(2)}) async-start(), calls=%async_computation.2 | async-start | bytes 1310720 | tf_op jit(solution)/shard_map/psum | solution.py:39
  124.0 112.6 %all-reduce.10.cloned.1.call-start = ((), (), s32[]{:S(2)}) async-start(), calls=%async_computation.3 | async-start | bytes 1310720 | tf_op jit(solution)/shard_map/psum | solution.py:39
  159.5 145.2 %all-reduce.12.cloned.1.call-start = ((), (), s32[]{:S(2)}) async-start(), calls=%async_computation.4 | async-start | bytes 1310720 | tf_op jit(solution)/shard_map/psum | solution.py:39
  271.0 110.6 %all-reduce.14.cloned.1.call-start = ((), (), s32[]{:S(2)}) async-start(), calls=%async_computation.5 | async-start | bytes 1310720 | tf_op jit(solution)/shard_map/psum | solution.py:39
Sparse Core Ops, SparseCore 0:
  30.8 28.6 all-reduce.5
  124.1 35.2 all-reduce.7
  162.9 73.6 all-reduce.9
  271.1 33.4 all-reduce.11
  308.0 73.6 all-reduce.13
